TPU v7x, 512 devices: a whole 4x4x16 slice. The times are simulated.
512 devices in a mesh: row: 32 (over z, core), col: 16 (over x, y).
Axes of the slice: x: 4, y: 4, z: 16, core: 2. Of those that a mesh axis runs over, the one named last changes fastest.
Arguments:
- view_left: bfloat16 [16384, 16384], P('row', 'col'), may hold values from -0.046875 to 0.046875
- view_right: bfloat16 [16384, 16384], P('row', 'col'), may hold values from -6 to 6
- view_product: bfloat16 [16384, 16384], P('row', 'col'), may hold values from -6 to 6
- delta_a_left: bfloat16 [16384, 512], P('row', 'col'), may hold values from -0.25 to 0.25
- delta_a_right: bfloat16 [16384, 512], P('row', 'col'), may hold values from -0.09375 to 0.09375
- delta_b_left: bfloat16 [16384, 512], P('col', 'row'), may hold values from -6 to 6
- delta_b_right: bfloat16 [16384, 512], P('col', 'row'), may hold values from -0.25 to 0.25
Outputs:
- updated_view: bfloat16 [16384, 16384], P('row', 'col')
All inputs are finite; a program needn't handle non-finite values.
Results may differ from a plain program's by a relative error of at most 0.005.
Values may be sent and summed in bfloat16 or wider, within the bound.
A program may use at most 64 MiB of HBM per device.

v0:
```python
import jax
import jax.numpy as jnp
from jax import lax
from jax.sharding import Mesh
from jax.sharding import PartitionSpec as P

COL = ("col_0", "col_1")
ROW = ("row_0", "row_1")


def gather_turned(arrays, axis, dims):
    turned = [jnp.moveaxis(a, dim, 0) for a, dim in zip(arrays, dims)]
    widths = [t[0].size for t in turned]
    both = jnp.concatenate([t.reshape(-1, w) for t, w in zip(turned, widths)], axis=1)
    result = lax.all_gather(both, axis, axis=0, tiled=True)
    pieces = jnp.split(result, [sum(widths[:k]) for k in range(1, len(widths))], axis=1)
    return tuple(
        (
            jnp.moveaxis(b.reshape(-1, *t.shape[1:]), 0, dim)
            for b, t, dim in zip(pieces, turned, dims)
        )
    )


def from_everyone(value, axis):
    copies = jnp.broadcast_to(value, (lax.axis_size(axis), *value.shape))
    return lax.all_to_all(copies, axis, split_axis=0, concat_axis=0, tiled=True)


def in_order(pieces, dim):
    pieces = jnp.moveaxis(pieces, 0, dim)
    lengths = pieces.shape
    return pieces.reshape(*lengths[:dim], lengths[dim] * lengths[dim + 1], *lengths[dim + 2 :])


def gather_axes(value, axes, dim):
    far, near = axes
    pieces = from_everyone(from_everyone(value, far), near)
    return in_order(pieces.swapaxes(0, 1).reshape(-1, *value.shape), dim)


def side_by_side(arrays, axis, dim, along):
    ends, at = ([], 0)
    for a in arrays[:-1]:
        at += a.shape[along]
        ends.append(at)
    both = jnp.concatenate(arrays, axis=along)
    return tuple(jnp.split(gather_axes(both, axis, dim), ends, axis=along))


def in_blocks(value, dim, devices):
    before, after = (value.shape[:dim], value.shape[dim + 1 :])
    return jnp.moveaxis(value.reshape(*before, devices, -1, *after), dim, 0)


def summed_on_arrival(value, axis, dim):
    pieces = in_blocks(value, dim, lax.axis_size(axis))
    arrived = lax.all_to_all(pieces, axis, split_axis=0, concat_axis=0, tiled=True)
    return arrived.sum(axis=0)


def summed_rows(value, axes, dim):
    far, near = axes
    pieces = in_blocks(value, dim, lax.axis_size(far))
    nearer = summed_on_arrival(pieces, near, dim + 1)
    arrived = lax.all_to_all(nearer, far, split_axis=0, concat_axis=0, tiled=True)
    return arrived.sum(axis=0)


def filled_up(lines, devices):
    spare = -lines.shape[0] % devices
    if not spare:
        return lines
    return jnp.concatenate([lines, jnp.zeros((spare, *lines.shape[1:]), lines.dtype)])


def sum_by_parts(value, axes):
    lines = value.reshape(-1, value.shape[-1])
    own = summed_rows(filled_up(lines, lax.axis_size(axes[0]) * lax.axis_size(axes[1])), axes, 0)
    whole = gather_axes(own, axes, 0)
    return whole[: len(lines)].reshape(value.shape)


def sum_in_order(pieces, axes, turns):
    lengths = [lax.axis_size(a) for a in axes]
    pieces = pieces.reshape(*lengths, *pieces.shape[1:])
    pieces = pieces.transpose(*turns, *range(len(axes), pieces.ndim))
    pieces = pieces.reshape(-1, *pieces.shape[len(axes) :])
    for k in turns:
        pieces = lax.psum_scatter(pieces, axes[k], scatter_dimension=0, tiled=True)
    return pieces[0]


def scatter_axes(value, axes, turns, dim):
    devices = lax.axis_size(axes)
    return sum_in_order(in_blocks(value, dim, devices), axes, turns)


def all_blocks(value, axes, turns):
    pieces = value[None]
    for k in turns:
        pieces = lax.all_gather(pieces, axes[k], axis=0, tiled=True)
    carried = [lax.axis_size(axes[k]) for k in reversed(turns)]
    pieces = pieces.reshape(*carried, *value.shape)
    turned = sorted(range(len(turns)), key=lambda place: turns[len(turns) - 1 - place])
    return pieces.transpose(*turned, *range(len(turns), pieces.ndim)).reshape(-1, *value.shape)


def gathered_by_axis(value, axes, turns, dim):
    return in_order(all_blocks(value, axes, turns), dim)


def collect(value, axis, dim):
    return in_order(from_everyone(value, axis), dim)


def contract_lead(first, second):
    return lax.dot_general(
        first, second, (((0,), (0,)), ((), ())), preferred_element_type=jnp.float32
    )


def contract_tail(first, second):
    return lax.dot_general(
        first, second, (((1,), (1,)), ((), ())), preferred_element_type=jnp.float32
    )


def per_device(
    view_left, view_right, view_product, delta_a_left, delta_a_right, delta_b_left, delta_b_right
):
    outer_u, inner_v = gather_turned((delta_a_left, delta_a_right), COL, (1, 1))
    inner_p, outer_q = side_by_side((delta_b_left, delta_b_right), ("row_0", "row_1"), 1, 0)
    rows_here = view_left.shape[0]
    cols_here = view_left.shape[1]
    stride_rows = lax.axis_size(ROW) // lax.axis_size(COL)
    offset = (lax.axis_index(ROW) - lax.axis_index(COL) * stride_rows) * rows_here
    inside = (offset >= 0) & (offset < cols_here)
    first_cell = jnp.clip(offset, 0, cols_here - rows_here)
    matched = lax.dynamic_slice_in_dim(inner_p, first_cell, rows_here, 0)
    cross_part = jnp.where(inside, contract_lead(inner_v, matched), 0.0)
    cross_total = sum_by_parts(cross_part, (("row_0", "row_1"), ("col_0", "col_1"))).astype(
        jnp.bfloat16
    )
    share_rows = inner_v.shape[1] // lax.axis_size(ROW)
    sliced = inner_v
    column_share = scatter_axes(contract_lead(sliced, view_right), ROW, (1, 0), 0)
    cross_rows = lax.dynamic_slice_in_dim(
        cross_total, lax.axis_index(ROW) * share_rows, share_rows, 0
    )
    weights_share = (column_share + contract_tail(cross_rows, outer_q)).astype(jnp.bfloat16)
    weights_w = gathered_by_axis(weights_share, ROW, (0, 1), 0)
    sliced = view_left
    row_share = summed_on_arrival(
        jnp.dot(sliced, inner_p, preferred_element_type=jnp.float32), COL, 0
    ).astype(jnp.bfloat16)
    projected = collect(row_share, COL, 0)
    updated = view_product.astype(jnp.float32) + jnp.dot(
        outer_u, weights_w, preferred_element_type=jnp.float32
    )
    updated = updated + contract_tail(projected, outer_q)
    return updated.astype(jnp.bfloat16)


def solution(mesh):
    split = Mesh(mesh.devices.reshape(16, 2, 4, 4), ("row_0", "row_1", "col_0", "col_1"))
    placed = (
        P(ROW, COL),
        P(ROW, COL),
        P(ROW, COL),
        P(ROW, COL),
        P(ROW, COL),
        P(COL, ROW),
        P(COL, ROW),
    )
    return jax.shard_map(
        per_device, mesh=split, in_specs=placed, out_specs=P(ROW, COL), check_vma=False
    )
```

profile of v0, /device:TPU:1, one launch (start us, length us, event | category | flops | bytes accessed | tf_op | source)
XLA Modules:
  0.0 252.6 jit_solution(16949043869651387830)
XLA Ops:
  6.5 1.5 pad_maximum_fusion
  8.1 0.8 pad_maximum_fusion.1
  8.8 1.1 broadcast_in_dim.22
  9.9 15.7 %all-to-all-start = ((bf16[16,2048,16]{1,2,0:T(8,128)(2,1)}), bf16[16,2048,16]{1,2,0:T(8,128)(2,1)S(1)}, u32[]{:S(2)}, u32[]{:S(2)}) async-start(bf16[16,2048,16]{1,2,0:T(8,128)(2,1)} %broadcast_in_dim.22), calls=%async_computation.2 | async-start | bytes 2097152 | tf_op jit(solution)/shard_map/all_to_all | solution.py:27
  25.7 46.2 %all-gather.4.cloned.1.call-done = bf16[512,1024]{1,0:T(8,128)(2,1)} async-done(((bf16[32,1024]{1,0:T(8,128)(2,1)}), bf16[512,1024]{1,0:T(8,128)(2,1)}) %all-gather.4.cloned.1.call-update) | async-done | bytes 1048592 | tf_op jit(solution)/shard_map/all_gather | solution.py:15
  71.9 1.8 fusion.5
  73.6 1.5 copy.13
  75.5 7.3 %all_to_all.43 = bf16[2,16,2048,16]{2,3,1,0:T(8,128)(2,1)S(1)} all-to-all(bf16[2,16,2048,16]{2,3,1,0:T(8,128)(2,1)S(1)} %broadcast_in_dim.23), channel_id=1, replica_groups=mesh['row_0'=16,'row_1'=2,'col_0'=4,'col_1'=4] {'row_1'}, dimensions={0} | all-to-all | bytes 4194304 | tf_op jit(solution)/shard_map/all_to_all | solution.py:27
  83.0 1.1 fusion.10
  84.2 13.2 %reduce-scatter.3.cloned.1.call-done = f32[16,16,1024]{2,1,0:T(8,128)} async-done(((f32[32,16,1024]{2,1,0:T(8,128)}), f32[16,16,1024]{2,1,0:T(8,128)}) %reduce-scatter.3.cloned.1.call-update) | async-done | bytes 1048592 | tf_op jit(solution)/shard_map/reduce_scatter | solution.py:90
  97.4 1.6 convolution_select_fusion
  99.0 0.6 copy.23
  99.7 21.8 %all_to_all.44 = f32[16,32,1,512]{3,1,2,0:T(8,128)S(1)} all-to-all(f32[16,32,1,512]{3,1,2,0:T(8,128)S(1)} %bitcast.47), channel_id=1, replica_groups=mesh['row_0'=16,'row_1'=2,'col_0'=4,'col_1'=4] {'col_0','col_1'}, dimensions={0} | all-to-all | bytes 2097152 | tf_op jit(solution)/shard_map/all_to_all | solution.py:58
  121.6 27.1 %all_to_all.45 = f32[32,1,512]{2,1,0:T(1,128)S(1)} all-to-all(f32[32,1,512]{2,1,0:T(1,128)S(1)} %reduce_sum.30), channel_id=1, replica_groups=mesh['row_0'=16,'row_1'=2,'col_0'=4,'col_1'=4] {'row_0','row_1'}, dimensions={0} | all-to-all | bytes 131072 | tf_op jit(solution)/shard_map/all_to_all | solution.py:66
  148.8 0.5 broadcast.4
  149.4 0.8 reduce.2
  150.2 16.2 %all_to_all.46 = bf16[32,2,256]{2,1,0:T(2,128)(2,1)S(1)} all-to-all(bf16[32,2,256]{2,1,0:T(2,128)(2,1)S(1)} %reshape.30), channel_id=1, replica_groups=mesh['row_0'=16,'row_1'=2,'col_0'=4,'col_1'=4] {'row_0','row_1'}, dimensions={0} | all-to-all | bytes 65536 | tf_op jit(solution)/shard_map/all_to_all | solution.py:27
  166.4 0.9 broadcast_in_dim.26
  167.3 5.1 %all-to-all-start.5 = ((bf16[16,32,1,512]{3,1,2,0:T(8,128)(2,1)}), bf16[16,32,1,512]{3,1,2,0:T(8,128)(2,1)S(1)}, u32[]{:S(2)}, u32[]{:S(2)}) async-start(bf16[16,32,1,512]{3,1,2,0:T(8,128)(2,1)} %broadcast_in_dim.26), calls=%async_computation.7 | async-start | bytes 1048576 | tf_op jit(solution)/shard_map/all_to_all | solution.py:27
  172.4 3.3 %fusion.11 = f32[512,512]{0,1:T(8,128)} fusion(bf16[1024,512]{0,1:T(8,128)(2,1)} %bitcast.54, bf16[512,1024]{1,0:T(8,128)(2,1)} %param.7), kind=kOutput, calls=%fused_computation.19 | convolution fusion | flops 536870912 | bytes 3145728 | tf_op jit(solution)/shard_map/dot_general | solution.py:155
  175.7 7.1 %all-to-all-done.5 = bf16[16,32,1,512]{3,1,2,0:T(8,128)(2,1)S(1)} async-done(((bf16[16,32,1,512]{3,1,2,0:T(8,128)(2,1)}), bf16[16,32,1,512]{3,1,2,0:T(8,128)(2,1)S(1)}, u32[]{:S(2)}, u32[]{:S(2)}) %all-to-all-start.5) | async-done | bytes 524320 | tf_op jit(solution)/shard_map/all_to_all | solution.py:27
  182.8 0.8 copy-done.1
  183.6 3.7 %all-to-all-start.6 = ((f32[16,32,512]{2,1,0:T(8,128)}), f32[16,32,512]{2,1,0:T(8,128)S(1)}, u32[]{:S(2)}, u32[]{:S(2)}) async-start(f32[16,32,512]{2,1,0:T(8,128)} %bitcast.50), calls=%async_computation.8 | async-start | bytes 2097152 | tf_op jit(solution)/shard_map/all_to_all | solution.py:58
  187.3 2.1 copy.22
  189.5 1.1 fusion
  190.6 25.3 %all-gather = bf16[256,1024]{1,0:T(8,128)(2,1)} all-gather(bf16[16,1024]{1,0:T(8,128)(2,1)S(1)} %fusion), channel_id=2, replica_groups=mesh['row_0'=16,'row_1'=2,'col_0'=4,'col_1'=4] {'row_0'}, dimensions={0}, use_global_device_ids=true | all-gather | bytes 557056 | tf_op jit(solution)/shard_map/all_gather | solution.py:102
  216.1 0.8 broadcast_in_dim.28
  216.9 6.3 %all-to-all-start.7 = ((bf16[16,32,512]{2,1,0:T(8,128)(2,1)}), bf16[16,32,512]{2,1,0:T(8,128)(2,1)S(1)}, u32[]{:S(2)}, u32[]{:S(2)}) async-start(bf16[16,32,512]{2,1,0:T(8,128)(2,1)} %broadcast_in_dim.28), calls=%async_computation.9 | async-start | bytes 1048576 | tf_op jit(solution)/shard_map/all_to_all | solution.py:27
  223.2 15.7 %all-gather.6.cloned.1.call-done = bf16[32,16,1024]{2,1,0:T(8,128)(2,1)} async-done(((bf16[16,16,1024]{2,1,0:T(8,128)(2,1)}), bf16[32,16,1024]{2,1,0:T(8,128)(2,1)}) %all-gather.6.cloned.1.call-update) | async-done | bytes 1048592 | tf_op jit(solution)/shard_map/all_gather | solution.py:102
  238.9 1.4 copy.17
  240.4 2.1 fusion.1
  242.5 3.5 %add_convert_fusion = bf16[512,1024]{1,0:T(8,128)(2,1)} fusion(f32[512,1024]{1,0:T(8,128)} %fusion.1, bf16[512,1024]{1,0:T(8,128)(2,1)} %param.9, bf16[512,512]{1,0:T(8,128)(2,1)S(1)} %bitcast.49, bf16[1024,512]{0,1:T(8,128)(2,1)S(1)} %bitcast.42), kind=kOutput, calls=%fused_computation | convolution fusion | flops 538968064 | bytes 5767168 | tf_op jit(solution)/shard_map/dot_general | solution.py:124
  (29 shorter events, 1.2 us)
Async XLA Ops:
  6.5 65.3 %copy-start = (bf16[512,1024]{1,0:T(8,128)(2,1)S(1)}, bf16[512,1024]{1,0:T(8,128)(2,1)}, u32[]{:S(2)}) copy-start(bf16[512,1024]{1,0:T(8,128)(2,1)} %param.8) | copy-start | bytes 3145732
  6.5 65.3 %all-gather.4.cloned.1.call-start = ((), (), s32[]{:S(2)}) async-start(), calls=%async_computation.10 | async-start | bytes 1114112 | tf_op jit(solution)/shard_map/all_gather | solution.py:15
  9.9 65.3 %all-to-all-start = ((bf16[16,2048,16]{1,2,0:T(8,128)(2,1)}), bf16[16,2048,16]{1,2,0:T(8,128)(2,1)S(1)}, u32[]{:S(2)}, u32[]{:S(2)}) async-start(bf16[16,2048,16]{1,2,0:T(8,128)(2,1)} %broadcast_in_dim.22), calls=%async_computation.2 | async-start | bytes 2097152 | tf_op jit(solution)/shard_map/all_to_all | solution.py:27
  25.7 71.7 %reduce-scatter.3.cloned.1.call-start = ((), (), s32[]{:S(2)}) async-start(), calls=%async_computation.11 | async-start | bytes 3145728 | tf_op jit(solution)/shard_map/reduce_scatter | solution.py:90
  75.1 114.4 %reduce-scatter.5.cloned.1.call-start = ((), (), s32[]{:S(2)}) async-start(), calls=%async_computation.12 | async-start | bytes 1114112 | tf_op jit(solution)/shard_map/reduce_scatter | solution.py:90
  83.0 14.4 %copy-start.2 = (bf16[512,1024]{1,0:T(8,128)(2,1)S(1)}, bf16[512,1024]{1,0:T(8,128)(2,1)}, u32[]{:S(2)}) copy-start(bf16[512,1024]{1,0:T(8,128)(2,1)} %all-gather.4.cloned.1.call-done) | copy-start | bytes 3145732
  167.3 15.5 %all-to-all-start.5 = ((bf16[16,32,1,512]{3,1,2,0:T(8,128)(2,1)}), bf16[16,32,1,512]{3,1,2,0:T(8,128)(2,1)S(1)}, u32[]{:S(2)}, u32[]{:S(2)}) async-start(bf16[16,32,1,512]{3,1,2,0:T(8,128)(2,1)} %broadcast_in_dim.26), calls=%async_computation.7 | async-start | bytes 1048576 | tf_op jit(solution)/shard_map/all_to_all | solution.py:27
  182.8 0.8 copy-start.1
  183.6 32.4 %all-to-all-start.6 = ((f32[16,32,512]{2,1,0:T(8,128)}), f32[16,32,512]{2,1,0:T(8,128)S(1)}, u32[]{:S(2)}, u32[]{:S(2)}) async-start(f32[16,32,512]{2,1,0:T(8,128)} %bitcast.50), calls=%async_computation.8 | async-start | bytes 2097152 | tf_op jit(solution)/shard_map/all_to_all | solution.py:58
  187.3 51.6 %all-gather.6.cloned.1.call-start = ((), (), s32[]{:S(2)}) async-start(), calls=%async_computation.13 | async-start | bytes 1572864 | tf_op jit(solution)/shard_map/all_gather | solution.py:102
  216.9 25.6 %all-to-all-start.7 = ((bf16[16,32,512]{2,1,0:T(8,128)(2,1)}), bf16[16,32,512]{2,1,0:T(8,128)(2,1)S(1)}, u32[]{:S(2)}, u32[]{:S(2)}) async-start(bf16[16,32,512]{2,1,0:T(8,128)(2,1)} %broadcast_in_dim.28), calls=%async_computation.9 | async-start | bytes 1048576 | tf_op jit(solution)/shard_map/all_to_all | solution.py:27
  238.9 1.5 copy-start.3
Sparse Core Ops, SparseCore 0:
  10.3 61.4 all-gather.3
  75.3 22.0 reduce-scatter.2
  100.2 63.1 reduce-scatter.4
  216.1 22.7 all-gather.5
where the time goes:
time: 254 us; the launch traced here: 253 us
  blocking collectives  97.8 us (39%)
  waiting for transfers between devices  82.2 us (32%)
  starting transfers between devices  31 us (12%)
  matrix products  13.3 us (5%)
  between operations  13.3 us (5%)
  local copies, waits for them, and re-layouts  11.7 us (5%)
  other arithmetic  3.29 us (1%)
    all_gather x1, waiting for transfers between devices, gather_turned(): result = lax.all_gather(both, axis, axis=0, tiled=True)  46.2 us
    all_to_all x3, starting transfers between devices, from_everyone(): return lax.all_to_all(copies, axis, split_axis=0, concat_axis=0, tiled=True)  27.2 us
    all_to_all x1, blocking collectives, summed_rows(): lax.all_to_all(nearer, far, split_axis=0, concat_axis=0, tiled=True)  27.1 us
    all_gather x1, blocking collectives, all_blocks(): pieces = lax.all_gather(pieces, axes[k], axis=0, tiled=True)  25.3 us
    all_to_all x2, blocking collectives, from_everyone(): return lax.all_to_all(copies, axis, split_axis=0, concat_axis=0, tiled=True)  23.5 us
    all_to_all x1, blocking collectives, summed_on_arrival(): lax.all_to_all(pieces, axis, split_axis=0, concat_axis=0, tiled=True)  21.8 us
    all_gather x1, waiting for transfers between devices, all_blocks(): pieces = lax.all_gather(pieces, axes[k], axis=0, tiled=True)  15.7 us
    reduce_scatter x2, waiting for transfers between devices, sum_in_order(): pieces = lax.psum_scatter(pieces, axes[k], scatter_dimension=0, tiled=True)  13.2 us
  transfers between devices with their start and end apart: 8, of which 4 were waited for; matrix products, arithmetic and copies ran while one was open for 9% of the time, Pallas kernels for 0%

commit v1 on v0

v1 whole, which is shorter than its diff:
```python
import functools

import jax
import jax.numpy as jnp
from jax import lax
from jax.experimental import pallas as pl
from jax.experimental.pallas import tpu as pltpu
from jax.sharding import Mesh
from jax.sharding import PartitionSpec as P

MESH = pl.DeviceIdType.MESH
F32 = jnp.float32
BF16 = jnp.bfloat16
NZ = 16
HALF = 256
NT = (((1,), (1,)), ((), ()))


def rem(a, n):
    return lax.rem(a + 2 * n, n)


def kernel(
    vt_h, ut_h, pt_h, qt_h, a_h, b_h, c_h, out_h,
    PT, QT, VT, UT, U, A, B, C, OUT,
    WOWN, WSND, WRCV, RSP, RRP, RSM, RRM, WT,
    CS, CIN, CR, DF, DS, R1, EF, ES, R2, PJ, ACC,
    load_sem, psem, psnd, qsem, qsnd, wsem, wsnd, xrcv, xsnd,
    rpr, rps, rmr, rms, vsem, vsnd, usem, usnd, crsem, crsnd,
    dsem, dsnd, jsem, jsnd, cinsem, csnd,
):
    z = lax.axis_index("z")
    k = lax.axis_index("k")
    x = lax.axis_index("x")
    y = lax.axis_index("y")
    sib = {"k": 1 - k}
    zp, zm = {"z": rem(z + 1, NZ)}, {"z": rem(z - 1, NZ)}
    pos = {"x": x, "y": y}
    pending = []

    def send(src, dst, ssem, rsem, dev):
        copy = pltpu.make_async_remote_copy(
            src_ref=src, dst_ref=dst, send_sem=ssem, recv_sem=rsem,
            device_id=dev, device_id_type=MESH,
        )
        copy.start()
        pending.append(copy)

    def recv(dst, rsem):
        pltpu.make_async_remote_copy(
            src_ref=dst, dst_ref=dst, send_sem=rsem, recv_sem=rsem,
            device_id=sib, device_id_type=MESH,
        ).wait_recv()

    loads = [
        pltpu.make_async_copy(pt_h, PT.at[2 * z + k], load_sem.at[0]),
        pltpu.make_async_copy(vt_h, VT.at[x, y], load_sem.at[1]),
        pltpu.make_async_copy(qt_h, QT.at[2 * z + k], load_sem.at[2]),
        pltpu.make_async_copy(ut_h, UT.at[x, y], load_sem.at[3]),
        pltpu.make_async_copy(b_h, B, load_sem.at[4]),
        pltpu.make_async_copy(a_h, A, load_sem.at[5]),
        pltpu.make_async_copy(c_h, C, load_sem.at[6]),
    ]
    for copy in loads:
        copy.start()

    barrier = pltpu.get_barrier_semaphore()
    peers = [zp, zm, sib]
    for axis in ("x", "y"):
        for step in (1, 3, 2):
            peers.append({axis: rem(pos[axis] + step, 4)})
    for dev in peers:
        pl.semaphore_signal(barrier, inc=1, device_id=dev, device_id_type=MESH)
    pl.semaphore_wait(barrier, len(peers))

    class ZGather:
        def __init__(self, buf, rsem, ssem, slot):
            self.buf, self.rsem, self.ssem, self.slot = buf, rsem, ssem, slot
            self.n = 0

        def out(self, ref, rs, dev):
            send(ref, ref, self.ssem.at[self.n], self.rsem.at[rs], dev)
            self.n += 1

        def start(self):
            own = self.buf.at[self.slot(z, k)]
            self.out(own, 0, zp)
            self.out(own, 8, zm)
            self.out(own, 16, sib)

        def step(self, s):
            ref = self.buf.at[self.slot(rem(z - 1 - s, NZ), k)]
            recv(ref, self.rsem.at[s])
            if s < 7:
                self.out(ref, s + 1, zp)
            self.out(ref, 17 + s, sib)
            if s < 7:
                ref = self.buf.at[self.slot(rem(z + 1 + s, NZ), k)]
                recv(ref, self.rsem.at[8 + s])
                if s < 6:
                    self.out(ref, 9 + s, zm)
                self.out(ref, 25 + s, sib)

        def finish(self):
            recv(self.buf.at[self.slot(z, 1 - k)], self.rsem.at[16])
            for s in range(8):
                recv(self.buf.at[self.slot(rem(z - 1 - s, NZ), 1 - k)], self.rsem.at[17 + s])
                if s < 7:
                    recv(self.buf.at[self.slot(rem(z + 1 + s, NZ), 1 - k)], self.rsem.at[25 + s])

    class PlaneGather:
        def __init__(self, buf, lanes, first, rsem, ssem, base):
            self.buf, self.lanes, self.first = buf, lanes, first
            self.rsem, self.ssem, self.base = rsem, ssem, base

        def view(self, phase, at):
            if phase == 0:
                spot = {**pos, self.first: at}
                return self.buf.at[spot["x"], spot["y"], :, self.lanes]
            if self.first == "x":
                return self.buf.at[:, at, :, self.lanes]
            return self.buf.at[at, :, :, self.lanes]

        def start(self, phase):
            axis = self.first if phase == 0 else ("y" if self.first == "x" else "x")
            mine = self.view(phase, pos[axis])
            for i, step in enumerate((1, 3, 2)):
                at = self.base + 3 * phase + i
                send(mine, mine, self.ssem.at[at], self.rsem.at[at], {axis: rem(pos[axis] + step, 4)})

        def wait(self, phase):
            axis = self.first if phase == 0 else ("y" if self.first == "x" else "x")
            for i, step in enumerate((1, 3, 2)):
                at = self.base + 3 * phase + i
                recv(self.view(phase, rem(pos[axis] - step, 4)), self.rsem.at[at])

    lanes = [pl.ds(0, HALF), pl.ds(HALF, HALF)]
    order = ["x", "y"]

    def halves(buf, rsem, ssem):
        return [PlaneGather(buf, lanes[h], order[h], rsem, ssem, 6 * h) for h in (0, 1)]

    gp = ZGather(PT, psem, psnd, lambda zz, kk: 2 * zz + kk)
    gq = ZGather(QT, qsem, qsnd, lambda zz, kk: 2 * zz + kk)
    gw = ZGather(WT, wsem, wsnd, lambda zz, kk: 16 * kk + zz)
    gv = halves(VT, vsem, vsnd)
    gu = halves(UT, usem, usnd)
    gc = halves(CR, crsem, crsnd)
    gj = halves(PJ, jsem, jsnd)

    def both(gathers, what, phase):
        for g in gathers:
            getattr(g, what)(phase)

    def rs_step(s):
        d = rem(z + 8 - s, NZ)
        total = WOWN[d]
        if s > 0:
            recv(RRP.at[s - 1], rpr.at[s - 1])
            total = total + RRP[s - 1].astype(F32)
        RSP[s] = total.astype(BF16)
        send(RSP.at[s], RRP.at[s], rps.at[s], rpr.at[s], zp)
        if s < 7:
            d = rem(z - 7 + s, NZ)
            total = WOWN[d]
            if s > 0:
                recv(RRM.at[s - 1], rmr.at[s - 1])
                total = total + RRM[s - 1].astype(F32)
            RSM[s] = total.astype(BF16)
            send(RSM.at[s], RRM.at[s], rms.at[s], rmr.at[s], zm)

    loads[0].wait()
    gp.start()
    loads[1].wait()
    both(gv, "start", 0)
    loads[2].wait()
    gq.start()
    loads[3].wait()

    gp.step(0)
    gq.step(0)
    both(gv, "wait", 0)
    both(gv, "start", 1)
    both(gu, "start", 0)
    gp.step(1)
    gq.step(1)
    gp.step(2)
    gq.step(2)
    both(gv, "wait", 1)
    both(gu, "wait", 0)
    both(gu, "start", 1)
    loads[4].wait()

    def partial_w(dst, which):
        rows = VT[pl.ds(2 * which, 2)].reshape(HALF, 512)

        @pl.loop(0, 4)
        def _(j):
            at = pl.ds(pl.multiple_of(j * HALF, HALF), HALF)
            dst[:, :, at] = jnp.dot(rows, B[:, at], preferred_element_type=F32).reshape(NZ, 16, HALF)

    partial_w(WSND, 1 - k)
    send(WSND, WRCV, xsnd, xrcv, sib)
    partial_w(WOWN, k)
    gp.step(3)
    gq.step(3)
    recv(WRCV, xrcv)
    WOWN[...] = WOWN[...] + WRCV[...]
    rs_step(0)
    gp.step(4)
    gq.step(4)
    rs_step(1)
    both(gu, "wait", 1)
    U[...] = UT[...].reshape(512, 512).T
    gp.step(5)
    gq.step(5)
    rs_step(2)
    gp.step(6)
    gq.step(6)
    rs_step(3)
    gp.step(7)
    gp.finish()

    diag = z == 4 * x + y

    def cross_copy(d, kk, n):
        zz = rem(z + d, NZ)
        return pltpu.make_async_remote_copy(
            src_ref=CS.at[kk, zz], dst_ref=CIN.at[k], send_sem=csnd.at[n], recv_sem=cinsem.at[k],
            device_id={"z": zz, "k": kk}, device_id_type=MESH,
        )

    @pl.when(diag)
    def _():
        cols = pl.ds(pl.multiple_of(512 * k, 512), 512)
        rows = VT[...].reshape(512, 512)
        part = lax.dot_general(rows, PT[:, :, cols].reshape(512, 512), NT, preferred_element_type=F32)
        CS[...] = part.astype(BF16).reshape(2, NZ, 16, 512)
        n = 0
        for d in (8, 7, 9, 6, 10, 5, 11, 4, 12, 3, 13, 2, 14, 1, 15):
            for kk in (0, 1):
                cross_copy(d, kk, n).start()
                n += 1
        pltpu.make_async_remote_copy(
            src_ref=CS.at[1 - k, z], dst_ref=CIN.at[k], send_sem=csnd.at[n], recv_sem=cinsem.at[k],
            device_id=sib, device_id_type=MESH,
        ).start()
        CIN[k] = CS[k, z]

    gq.step(7)
    loads[5].wait()
    rs_step(4)

    points = PT[...].reshape(512, 1024)
    for i in range(4):
        part = lax.dot_general(A[pl.ds(128 * i, 128), :], points, NT, preferred_element_type=F32)
        part = part.reshape(4, 32, 512)
        DF[i] = part
        DS[i] = part.astype(BF16)

    def d_start(phase):
        for h in (0, 1):
            axis = order[h] if phase == 0 else order[1 - h]
            for i, step in enumerate((1, 3, 2)):
                t = rem(pos[axis] + step, 4)
                at = 6 * h + 3 * phase + i
                if phase == 1:
                    src, dst = ES.at[h, t], R2.at[h, i]
                else:
                    src = DS.at[t, :, :, lanes[h]] if h == 0 else DS.at[:, t, :, lanes[h]]
                    dst = R1.at[h, i]
                send(src, dst, dsnd.at[at], dsem.at[at], {axis: t})

    def d_first():
        for h in (0, 1):
            for i in range(3):
                recv(R1.at[h, i], dsem.at[6 * h + i])
            total = DF[x, :, :, lanes[h]] if h == 0 else DF[:, y, :, lanes[h]]
            for i in range(3):
                total = total + R1[h, i].astype(F32)
            EF[h] = total
            ES[h] = total.astype(BF16)
        d_start(1)

    def d_second():
        for h in (0, 1):
            for i in range(3):
                recv(R2.at[h, i], dsem.at[6 * h + 3 + i])
            total = EF[h, pos[order[1 - h]]]
            for i in range(3):
                total = total + R2[h, i].astype(F32)
            PJ[x, y, :, lanes[h]] = total.astype(BF16)

    d_start(0)
    rs_step(5)

    @pl.when(jnp.logical_not(diag))
    def _():
        for j in (0, 1):
            recv(CIN.at[j], cinsem.at[j])

    @pl.when(diag)
    def _():
        recv(CIN.at[1 - k], cinsem.at[1 - k])

    CR[x, y] = (CIN[0].astype(F32) + CIN[1].astype(F32)).astype(BF16)
    both(gc, "start", 0)
    rs_step(6)
    d_first()
    both(gc, "wait", 0)
    both(gc, "start", 1)
    rs_step(7)
    d_second()
    both(gj, "start", 0)
    gq.finish()
    both(gc, "wait", 1)
    cross = jnp.sum(CR[...].astype(F32).reshape(16, 16, 512), axis=0).astype(BF16)
    term = jnp.dot(cross, QT[...].reshape(512, 1024), preferred_element_type=F32)
    recv(RRP.at[7], rpr.at[7])
    recv(RRM.at[6], rmr.at[6])
    total = WOWN[z] + RRP[7].astype(F32) + RRM[6].astype(F32)
    WT[16 * k + z] = (total + term).astype(BF16)
    gw.start()
    both(gj, "wait", 0)
    both(gj, "start", 1)
    gw.step(0)
    gw.step(1)
    gw.step(2)
    both(gj, "wait", 1)
    gw.step(3)
    loads[6].wait()

    def tiles(dst, base, left, right):
        @pl.loop(0, 4)
        def _(j):
            at = pl.ds(pl.multiple_of(j * HALF, HALF), HALF)
            weights = right[:, :, at].reshape(512, HALF)
            part = jnp.dot(left, weights, preferred_element_type=F32)
            dst[:, at] = (base[:, at].astype(F32) + part).astype(dst.dtype)

    tiles(ACC, C, PJ[...].reshape(512, 512), QT)
    for s in range(4, 8):
        gw.step(s)
    gw.finish()
    tiles(OUT, ACC, U[...], WT)
    store = pltpu.make_async_copy(OUT, out_h, load_sem.at[7])
    store.start()
    for copy in pending:
        copy.wait_send()

    @pl.when(diag)
    def _():
        n = 0
        for d in (8, 7, 9, 6, 10, 5, 11, 4, 12, 3, 13, 2, 14, 1, 15):
            for kk in (0, 1):
                cross_copy(d, kk, n).wait_send()
                n += 1
        pltpu.make_async_remote_copy(
            src_ref=CS.at[1 - k, z], dst_ref=CIN.at[k], send_sem=csnd.at[n], recv_sem=cinsem.at[k],
            device_id=sib, device_id_type=MESH,
        ).wait_send()

    store.wait()


def per_device(a, b, c, u, v, p, q):
    dma = pltpu.SemaphoreType.DMA
    anywhere = pl.BlockSpec(memory_space=pl.ANY)
    vm = pltpu.VMEM
    scratch = [
        vm((32, 16, 1024), BF16),
        vm((32, 16, 1024), BF16),
        vm((4, 4, 32, 512), BF16),
        vm((4, 4, 32, 512), BF16),
        vm((512, 512), BF16),
        vm((512, 1024), BF16),
        vm((512, 1024), BF16),
        vm((512, 1024), BF16),
        vm((512, 1024), BF16),
        vm((16, 16, 1024), F32),
        vm((16, 16, 1024), F32),
        vm((16, 16, 1024), F32),
        vm((8, 16, 1024), BF16),
        vm((8, 16, 1024), BF16),
        vm((7, 16, 1024), BF16),
        vm((7, 16, 1024), BF16),
        vm((32, 16, 1024), BF16),
        vm((2, 16, 16, 512), BF16),
        vm((2, 16, 512), BF16),
        vm((4, 4, 16, 512), BF16),
        vm((4, 4, 32, 512), F32),
        vm((4, 4, 32, 512), BF16),
        vm((2, 3, 4, 32, HALF), BF16),
        vm((2, 4, 32, HALF), F32),
        vm((2, 4, 32, HALF), BF16),
        vm((2, 3, 32, HALF), BF16),
        vm((4, 4, 32, 512), BF16),
        vm((512, 1024), F32),
        dma((8,)),
        dma((32,)), dma((31,)),
        dma((32,)), dma((31,)),
        dma((32,)), dma((31,)),
        dma, dma,
        dma((8,)), dma((8,)),
        dma((7,)), dma((7,)),
        dma((12,)), dma((12,)),
        dma((12,)), dma((12,)),
        dma((12,)), dma((12,)),
        dma((12,)), dma((12,)),
        dma((12,)), dma((12,)),
        dma((2,)), dma((31,)),
    ]
    return pl.pallas_call(
        kernel,
        out_shape=jax.ShapeDtypeStruct(c.shape, c.dtype),
        in_specs=[anywhere] * 7,
        out_specs=anywhere,
        scratch_shapes=scratch,
        compiler_params=pltpu.CompilerParams(
            collective_id=0, has_side_effects=True, vmem_limit_bytes=48 * 1024 * 1024
        ),
        name="maintain",
    )(v.T, u.T, p.T, q.T, a, b, c)


def solution(mesh):
    split = Mesh(mesh.devices.reshape(NZ, 2, 4, 4), ("z", "k", "x", "y"))
    row, col = ("z", "k"), ("x", "y")
    placed = (
        P(row, col), P(row, col), P(row, col), P(row, col), P(row, col), P(col, row), P(col, row),
    )
    return jax.shard_map(
        per_device, mesh=split, in_specs=placed, out_specs=P(row, col), check_vma=False
    )
```

time: 254 us -> 97.2 us (0.38)
  blocking collectives: 97.8 us -> 0 us
  Pallas kernels: 0 us -> 89 us
  waiting for transfers between devices: 82.2 us -> 0 us
  starting transfers between devices: 31 us -> 0 us
  matrix products: 13.3 us -> 0 us
  between operations: 13.3 us -> 0.02 us
  local copies, waits for them, and re-layouts: 11.7 us -> 7.67 us
  other arithmetic: 3.29 us -> 0 us
    pallas_call x0 -> x1, Pallas kernels: none -> 89 us  [per_device(): pl.pallas_call(kernel, out_shape=jax.ShapeDtypeStruct(c.shape, c.dtype),...]
    all_to_all x4 -> x0, blocking collectives: 72.4 us -> none  [the longest x1 27.1 us: summed_rows(): lax.all_to_all(nearer, far, split_axis=0, concat_axis=0, tiled=True)]
    all_gather x2 -> x0, waiting for transfers between devices: 61.8 us -> none  [the longest x1 46.2 us: gather_turned(): result = lax.all_gather(both, axis, axis=0, tiled=True)]
    all_to_all x4 -> x0, starting transfers between devices: 30.9 us -> none  [the longest x3 27.2 us: from_everyone(): return lax.all_to_all(copies, axis, split_axis=0, concat_axis=0, tiled=True)]
    all_gather x1 -> x0, blocking collectives: 25.3 us -> none  [all_blocks(): pieces = lax.all_gather(pieces, axes[k], axis=0, tiled=True)]
    dot_general x6 -> x0, matrix products: 13.3 us -> none  [the longest x2 4.65 us: contract_tail(): lax.dot_general(first, second, (((1,), (1,)), ((), ())), preferred_elemen...]
    reduce_scatter x2 -> x0, waiting for transfers between devices: 13.2 us -> none  [sum_in_order(): pieces = lax.psum_scatter(pieces, axes[k], scatter_dimension=0, tiled=True)]
    all_to_all x4 -> x0, waiting for transfers between devices: 7.12 us -> none  [the longest x3 7.12 us: from_everyone(): return lax.all_to_all(copies, axis, split_axis=0, concat_axis=0, tiled=True)]
  transfers between devices with their start and end apart: 8 -> 0, of which waited for: 4 -> 0; matrix products, arithmetic and copies ran while one was open for 9% -> 0% of each run, Pallas kernels for 0% -> 0%
where the time goes in v1:
time: 97.2 us; the launch traced here: 96.7 us
  Pallas kernels  89 us (92%)
  local copies, waits for them, and re-layouts  7.67 us (8%)
    pallas_call x1, Pallas kernels, per_device(): pl.pallas_call(kernel, out_shape=jax.ShapeDtypeStruct(c.shape, c.dtype),...  89 us
    unnamed x15, local copies, waits for them, and re-layouts  7.67 us

profile of v1, /device:TPU:1, one launch (start us, length us, event | category | flops | bytes accessed | tf_op | source)
XLA Modules:
  0.0 96.7 jit_solution(13430301119364773621)
XLA Ops:
  0.0 0.0 copy-start
  0.0 1.2 %copy-done = bf16[512,1024]{1,0:T(8,128)(2,1)S(1)} copy-done((bf16[512,1024]{1,0:T(8,128)(2,1)S(1)}, bf16[512,1024]{1,0:T(8,128)(2,1)}, u32[]{:S(2)}) %copy-start) | copy-done | bytes 1048600
  1.2 0.0 copy-start.1
  1.2 1.2 %copy-done.1 = bf16[512,1024]{1,0:T(8,128)(2,1)S(1)} copy-done((bf16[512,1024]{1,0:T(8,128)(2,1)S(1)}, bf16[512,1024]{1,0:T(8,128)(2,1)}, u32[]{:S(2)}) %copy-start.1) | copy-done | bytes 1048600
  2.5 0.0 copy-start.2
  2.5 1.2 %copy-done.2 = bf16[512,1024]{1,0:T(8,128)(2,1)S(1)} copy-done((bf16[512,1024]{1,0:T(8,128)(2,1)S(1)}, bf16[512,1024]{1,0:T(8,128)(2,1)}, u32[]{:S(2)}) %copy-start.2) | copy-done | bytes 1048600
  3.7 0.0 copy-start.3
  3.7 0.8 copy-done.3
  4.4 0.0 copy-start.4
  4.4 0.8 copy-done.4
  5.2 0.0 copy-start.5
  5.2 0.8 copy-done.5
  6.0 0.0 copy-start.6
  6.0 0.8 copy-done.6
  6.7 89.0 %maintain.1 = bf16[512,1024]{1,0:T(8,128)(2,1)S(1)} custom-call(bf16[32,512]{1,0:T(8,128)(2,1)S(1)} %bitcast.4, bf16[32,512]{1,0:T(8,128)(2,1)S(1)} %bitcast.5, bf16[16,1024]{1,0:T(8,128)(2,1)S(1)} %bitcast.6, bf16[16,1024]{1,0:T(8,128)(2,1)S(1)} %bitcast.7, bf16[512,1024]{1,0:T(8,128)(2,1)S(1)} %copy-done, bf16[512,1024]{1,0:T(8,128)(2,1)S(1)} %copy-done.1, ...), custom_call_target="tpu_custom_call" | custom-call | tf_op jit(solution)/shard_map/maintain/pallas_call | solution.py:413
  95.7 1.0 %copy.9 = bf16[512,1024]{1,0:T(8,128)(2,1)} copy(bf16[512,1024]{1,0:T(8,128)(2,1)S(1)} %maintain.1) | data formatting | bytes 2097152
Async XLA Ops:
  0.0 1.2 %copy-start = (bf16[512,1024]{1,0:T(8,128)(2,1)S(1)}, bf16[512,1024]{1,0:T(8,128)(2,1)}, u32[]{:S(2)}) copy-start(bf16[512,1024]{1,0:T(8,128)(2,1)} %a_h.1) | copy-start | bytes 3145732
  1.2 1.2 %copy-start.1 = (bf16[512,1024]{1,0:T(8,128)(2,1)S(1)}, bf16[512,1024]{1,0:T(8,128)(2,1)}, u32[]{:S(2)}) copy-start(bf16[512,1024]{1,0:T(8,128)(2,1)} %b_h.1) | copy-start | bytes 3145732
  2.5 1.2 %copy-start.2 = (bf16[512,1024]{1,0:T(8,128)(2,1)S(1)}, bf16[512,1024]{1,0:T(8,128)(2,1)}, u32[]{:S(2)}) copy-start(bf16[512,1024]{1,0:T(8,128)(2,1)} %c_h.1) | copy-start | bytes 3145732
  3.7 0.8 copy-start.3
  4.4 0.8 copy-start.4
  5.2 0.8 copy-start.5
  6.0 0.8 copy-start.6

commit v2 on v0

v2 whole, which is shorter than its diff:
```python
import jax
import jax.numpy as jnp
from jax import lax
from jax.experimental import pallas as pl
from jax.experimental.pallas import tpu as pltpu
from jax.sharding import Mesh
from jax.sharding import PartitionSpec as P

MESH = pl.DeviceIdType.MESH
F32 = jnp.float32
BF16 = jnp.bfloat16
NZ = 16
HALF = 256
NT = (((1,), (1,)), ((), ()))
STEPS = (1, 3, 2)


def rem(a, n):
    return lax.rem(a + 2 * n, n)


def kernel(
    vt_h, ut_h, pt_h, qt_h, a_h, b_h, c_h, OUT,
    PT, QT, VT, VS, UU, UN, U, A, AX, B, BX, C, W,
    RSP, RRP, RSM, RRM, LSP, LRP, LSM, LRM, WT,
    XV, CR, DF, DS, R1, EF, ES, R2, PJ, PN, ACC,
    load_sem, xrcv, xsnd, psem, psnd, pfwd, qsem, qsnd, qfwd, wsem, wsnd, wfwd, phalf,
    rpr, rmr, lpr, lmr, rsnd, vsem, vsnd, usem, usnd, crsem, crsnd,
    dsem, dsnd, jsem, jsnd, scsem, scsnd, scfar, free, known, told,
):
    z = lax.axis_index("z")
    k = lax.axis_index("k")
    x = lax.axis_index("x")
    y = lax.axis_index("y")
    sib = {"k": 1 - k}
    zp, zm = {"z": rem(z + 1, NZ)}, {"z": rem(z - 1, NZ)}
    zpp, zmm = {"z": rem(z + 2, NZ)}, {"z": rem(z - 2, NZ)}
    pos = {"x": x, "y": y}
    diag = z == 4 * x + y

    def send(src, dst, ssem, rsem, dev):
        pltpu.make_async_remote_copy(
            src_ref=src, dst_ref=dst, send_sem=ssem, recv_sem=rsem,
            device_id=dev, device_id_type=MESH,
        ).start()

    def recv(dst, rsem):
        pltpu.make_async_remote_copy(
            src_ref=dst, dst_ref=dst, send_sem=rsem, recv_sem=rsem,
            device_id=sib, device_id_type=MESH,
        ).wait_recv()

    def sent(ref, ssem):
        pltpu.make_async_remote_copy(
            src_ref=ref, dst_ref=ref, send_sem=ssem, recv_sem=ssem,
            device_id=sib, device_id_type=MESH,
        ).wait_send()

    low, high = pl.ds(0, 512), pl.ds(512, 512)
    own_lanes = pl.ds(pl.multiple_of(512 * k, 512), 512)
    loads = [
        pltpu.make_async_copy(pt_h, PT.at[z, k], load_sem.at[0]),
        pltpu.make_async_copy(vt_h, VT.at[x, y, :, own_lanes], load_sem.at[1]),
        pltpu.make_async_copy(qt_h, QT.at[z, k], load_sem.at[2]),
        pltpu.make_async_copy(ut_h, UU.at[x, y, k], load_sem.at[3]),
        pltpu.make_async_copy(b_h, B, load_sem.at[4]),
        pltpu.make_async_copy(a_h, A, load_sem.at[5]),
        pltpu.make_async_copy(c_h, C, load_sem.at[6]),
    ]
    for copy in loads:
        copy.start()

    barrier = pltpu.get_barrier_semaphore()
    near = [zp, zm, zpp, zmm]
    for axis in ("x", "y"):
        for step in STEPS:
            near.append({axis: rem(pos[axis] + step, 4)})
    peers = [sib] + [{**dev, "k": kk} for dev in near for kk in (0, 1)]
    for dev in peers:
        pl.semaphore_signal(barrier, inc=1, device_id=dev, device_id_type=MESH)
    pl.semaphore_wait(barrier, len(peers))

    class ZWide:
        def __init__(self, buf, rsem, ssem, fwd, part=slice(None)):
            self.buf, self.rsem, self.ssem, self.fwd, self.part = buf, rsem, ssem, fwd, part

        def at(self, d):
            return self.buf.at[rem(z - d, NZ), self.part]

        def place(self, d):
            return d - 1 if d > 0 else 7 - d

        def out(self, ref, d):
            dev = {1: zp, 2: zpp, -1: zm, -2: zmm}[d if abs(d) < 3 else (2 - d % 2) * (1 if d > 0 else -1)]
            send(ref, ref, self.ssem, self.rsem.at[self.place(d)], dev)

        def arrive(self, d):
            ref = self.at(d)
            recv(ref, self.rsem.at[self.place(d)])
            return ref

        def share(self, d):
            ref = self.at(d)
            send(ref, ref, self.ssem, self.fwd.at[0 if abs(d) < 6 else 1], sib)

        def own(self):
            return self.at(0)

        def start(self):
            self.out(self.own(), 2)
            self.out(self.own(), -2)

        def leaves(self, j):
            for sign in (1, -1):
                self.out(self.at(2 * j * sign) if j else self.own(), (2 * j + 1) * sign)

        def hub(self, j):
            self.on(j)
            self.off(j)

        def on(self, j):
            for sign, most in ((1, 8), (-1, 7)):
                d = 2 * j * sign
                ref = self.arrive(d)
                if 2 * j + 2 <= most:
                    self.out(ref, d + 2 * sign)

        def off(self, j):
            self.leaves(j - 1)
            if j == 3:
                self.leaves(3)
            self.share(2 * j)
            self.share(-2 * j)

        def leaf(self, j):
            for sign in (1, -1):
                d = (2 * j + 1) * sign
                self.arrive(d)
                self.share(d)

        def last(self):
            self.arrive(8)
            self.share(8)

        def shared(self, group):
            recv(self.buf.at[pl.ds(0, 5 if group else 10), self.part], self.fwd.at[group])

        def done(self):
            sent(self.buf.at[pl.ds(0, 15)], self.ssem)

    class ZNear(ZWide):
        def out(self, ref, d):
            send(ref, ref, self.ssem, self.rsem.at[self.place(d)], zp if d > 0 else zm)

        def start(self):
            self.leaves(0)

        def step(self, s):
            for sign, most in ((1, 8), (-1, 7)):
                if s < most:
                    d = sign * (s + 1)
                    ref = self.arrive(d)
                    if s + 1 < most:
                        self.out(ref, d + sign)
                    self.share(d)

    class ZHalves(ZWide):
        def own(self):
            return self.buf.at[z, k]

        def out(self, ref, d):
            if abs(d) > 2:
                super().out(ref, d)
                return
            dev = {1: zp, 2: zpp, -1: zm, -2: zmm}[d]
            place = 4 * k + {1: 0, 2: 1, -1: 2, -2: 3}[d]
            send(ref, ref, self.ssem, phalf.at[place], {**dev, "k": 1})

        def arrive(self, d):
            if abs(d) > 2:
                return super().arrive(d)
            for kk in (0, 1):
                recv(self.buf.at[rem(z - d, NZ), kk], phalf.at[4 * kk + {1: 0, 2: 1, -1: 2, -2: 3}[d]])
            return self.at(d)

        def done(self):
            sent(W.at[pl.ds(0, 14)], self.ssem)

    class PlaneGather:
        def __init__(self, buf, lanes, first, rsem, ssem, base, to):
            self.buf, self.lanes, self.first = buf, lanes, first
            self.rsem, self.ssem, self.base = rsem, ssem, base
            self.mid = (slice(None),) * (len(buf.shape) - 3)
            self.to = to

        def view(self, phase, at):
            if phase == 0:
                spot = {**pos, self.first: at}
                return self.buf.at[(spot["x"], spot["y"], *self.mid, self.lanes)]
            if self.first == "x":
                return self.buf.at[(slice(None), at, *self.mid, self.lanes)]
            return self.buf.at[(at, slice(None), *self.mid, self.lanes)]

        def axis(self, phase):
            return self.first if phase == 0 else ("y" if self.first == "x" else "x")

        def start(self, phase):
            axis = self.axis(phase)
            mine = self.view(phase, pos[axis])
            for step in STEPS:
                dev = {axis: rem(pos[axis] + step, 4), **self.to}
                send(mine, mine, self.ssem.at[phase], self.rsem.at[self.base + phase], dev)

        def wait(self, phase):
            some = (pl.ds(0, 3), slice(None)) if phase else (0, pl.ds(0, 3))
            recv(self.buf.at[(*some, *self.mid, self.lanes)], self.rsem.at[self.base + phase])

    lanes = [pl.ds(0, HALF), pl.ds(HALF, HALF)]
    order = ["x", "y"]

    def halves(buf, rsem, ssem, cut=lanes, to={}):
        return [PlaneGather(buf, cut[h], order[h], rsem, ssem, 2 * h, to) for h in (0, 1)]

    def plane_done(buf, ssem):
        sent(buf.at[0, pl.ds(0, 3)], ssem.at[0])
        sent(buf.at[pl.ds(0, 3)], ssem.at[1])

    gp = ZHalves(PT, psem, psnd, pfwd)
    gw = [ZWide(WT, wsem.at[i], wsnd.at[i], wfwd.at[i], i) for i in (0, 1)]
    gq = [ZNear(QT, qsem.at[i], qsnd.at[i], qfwd.at[i], i) for i in (0, 1)]
    gv = halves(VT, vsem, vsnd, [low, high], {"k": 1})
    gu = halves(UU, usem, usnd)
    gc = halves(CR, crsem, crsnd)
    gj = halves(PJ, jsem, jsnd)

    def both(gathers, what, phase):
        for g in gathers:
            getattr(g, what)(phase)

    def tiles(dst, base, left, right):
        for j in range(4):
            at = pl.ds(j * HALF, HALF)
            weights = right[..., at].reshape(512, HALF)
            part = jnp.dot(left, weights, preferred_element_type=F32)
            dst[:, at] = (base[:, at].astype(F32) + part).astype(dst.dtype)

    def rs_out(d, parts, src, dst, rsem, i, dev):
        total = W[d]
        for ref, sem, n in parts:
            recv(ref.at[n], sem.at[n])
            total = total + ref[n].astype(F32)
        src[i] = total.astype(BF16)
        send(src.at[i], dst.at[i], rsnd, rsem.at[i], dev)

    def rs_plus(i):
        parts = [(LRP, lpr, i - 1), (RRP, rpr, i - 1)] if i else []
        rs_out(rem(z + 8 - 2 * i, NZ), parts, RSP, RRP, rpr, i, zpp)

    def rs_minus(i):
        parts = [(LRM, lmr, i)] + ([(RRM, rmr, i - 1)] if i else [])
        rs_out(rem(z - 6 + 2 * i, NZ), parts, RSM, RRM, rmr, i, zmm)

    def rs_leaf(i):
        rs_out(rem(z - 7 + 2 * i, NZ), [], LSM, LRM, lmr, i, zm)
        rs_out(rem(z + 7 - 2 * i, NZ), [], LSP, LRP, lpr, i, zp)

    def sum_w():
        left = VT[...].reshape(512, 1024)
        for j in range(4):
            at = pl.ds(j * HALF, HALF)
            part = jnp.dot(left[:, :512], BX[:, at], preferred_element_type=F32)
            part = part + jnp.dot(left[:, 512:], B[:, at], preferred_element_type=F32)
            W[:, :, at] = part.reshape(NZ, 32, HALF)

    def cross_part():
        part = lax.dot_general(XV[...], PT[...].reshape(512, 1024), NT, preferred_element_type=F32)
        CR[x, y] = part.astype(BF16)

    def own_w():
        cross = jnp.sum(CR[...].astype(F32).reshape(16, 32, 512), axis=0).astype(BF16)
        total = W[z] + jnp.dot(cross, QT[...].reshape(512, 1024), preferred_element_type=F32)
        for ref, sem, n in ((LRP, lpr, 3), (LRM, lmr, 3), (RRP, rpr, 3), (RRM, rmr, 2)):
            recv(ref.at[n], sem.at[n])
            total = total + ref[n].astype(F32)
        WT[z] = total.astype(BF16).reshape(2, 16, 1024)

    def w_start():
        for g in gw:
            g.start()

    def w_hub(j):
        for g in gw:
            g.on(j)
        for g in gw:
            g.off(j)

    def w_leaf(j):
        for g in gw:
            g.leaf(j)

    def w_last():
        for g in gw:
            g.last()

    def q_step(s):
        for g in gq:
            g.step(s)

    def tell(i):
        pl.semaphore_signal(told.at[i], inc=1, device_id=zpp, device_id_type=MESH)
        pl.semaphore_signal(told.at[3 + i], inc=1, device_id=zmm, device_id_type=MESH)

    def hear(i):
        pl.semaphore_wait(told.at[i], 1)
        pl.semaphore_wait(told.at[3 + i], 1)

    far = (8, 7, 9, 6, 10, 5, 11)
    close = (4, 12, 3, 13, 2, 14, 1, 15, 0)

    def scatter_some(some, src, ssem):
        for d in some:
            zz = rem(z + d, NZ)
            send(src.at[zz // 4, lax.rem(zz, 4)], XV, ssem, scsem, {"z": zz, "k": 1})

    def pass_v():
        return pltpu.make_async_remote_copy(
            src_ref=VT, dst_ref=VS, send_sem=xsnd.at[3], recv_sem=xrcv.at[3],
            device_id=sib, device_id_type=MESH,
        )

    @pl.when(k == 1)
    def _():
        loads[1].wait()
        gv[1].start(0)
        loads[0].wait()
        gp.start()
        loads[2].wait()
        send(QT.at[z, 1], QT.at[z, 1], xsnd.at[0], xrcv.at[0], sib)
        loads[3].wait()
        send(UU.at[x, y, 1], UU.at[x, y, 1], xsnd.at[1], xrcv.at[1], sib)
        send(PT.at[z, 1], PT.at[z, 1], xsnd.at[5], xrcv.at[5], sib)
        send(a_h, AX, xsnd.at[2], xrcv.at[2], sib)
        gv[1].wait(0)
        gv[1].start(1)
        recv(VT.at[x, y, :, low], xrcv.at[1])
        gv[0].wait(0)
        gv[0].start(1)
        gp.hub(1)
        gp.hub(2)
        gp.leaf(0)
        gv[1].wait(1)
        gv[0].wait(1)

        pl.semaphore_wait(known, 1)

        @pl.when(diag)
        def _():
            pass_v().start()
            scatter_some(far, VT, scfar)

        loads[4].wait()
        recv(BX, xrcv.at[2])
        sum_w()
        rs_plus(0)
        rs_leaf(0)
        gp.hub(3)
        gp.leaf(1)
        gp.leaf(2)
        rs_minus(0)
        rs_leaf(1)
        gp.last()
        gp.leaf(3)
        rs_plus(1)
        rs_minus(1)
        rs_leaf(2)
        recv(PT.at[z, 0], xrcv.at[0])
        recv(XV, scsem)
        cross_part()
        both(gc, "start", 0)
        rs_plus(2)
        rs_minus(2)
        rs_leaf(3)
        both(gc, "wait", 0)
        both(gc, "start", 1)
        rs_plus(3)
        recv(QT.at[z, 0], xrcv.at[5])
        for g in gq:
            g.shared(0)
            g.shared(1)
        both(gc, "wait", 1)
        pl.semaphore_signal(free, inc=1, device_id=sib, device_id_type=MESH)
        own_w()
        w_start()
        send(WT.at[z], WT.at[z], xsnd.at[4], xrcv.at[4], sib)
        w_hub(1)
        w_hub(2)
        w_leaf(0)
        loads[6].wait()
        loads[5].wait()
        recv(UN, xrcv.at[4])
        U[...] = UN[...].reshape(512, 512).T
        w_hub(3)
        w_leaf(1)
        for h in (0, 1):
            recv(PN.at[:, :, :, lanes[h]], xrcv.at[6 + h])
        tiles(ACC, C, PN[...].reshape(512, 512), QT)
        w_leaf(2)
        w_last()
        w_leaf(3)
        tiles(OUT, ACC, U[...], WT)
        gp.done()
        for g in gw:
            g.done()
        sent(PT.at[pl.ds(0, 15)], rsnd)
        sent(VT.at[0, pl.ds(0, 3), :, low], vsnd.at[0])
        sent(VT.at[pl.ds(0, 3)], vsnd.at[1])
        plane_done(CR, crsnd)
        sent(QT.at[z, 1], xsnd.at[0])
        sent(UU.at[x, y, 1], xsnd.at[1])
        sent(AX, xsnd.at[2])
        sent(WT.at[z], xsnd.at[4])
        sent(PT.at[z, 1], xsnd.at[5])

        @pl.when(diag)
        def _():
            pass_v().wait_send()
            sent(PT.at[pl.ds(0, 7)], scfar)


    def d_part(h):
        points = PT[pl.ds(8 * h, 8)].reshape(HALF, 1024)
        for r, left in ((0, A), (1, AX)):
            part = lax.dot_general(left[...], points, NT, preferred_element_type=F32).reshape(4, 4, 32, HALF)
            DF[:, :, r, :, lanes[h]] = part
            DS[:, :, r, :, lanes[h]] = part.astype(BF16)

    def d_start(h, phase):
        axis = order[h] if phase == 0 else order[1 - h]
        for i, step in enumerate(STEPS):
            t = rem(pos[axis] + step, 4)
            if phase == 1:
                src, dst = ES.at[h, t], R2.at[h, i]
            else:
                src = DS.at[t, :, :, :, lanes[h]] if h == 0 else DS.at[:, t, :, :, lanes[h]]
                dst = R1.at[h, i]
            send(src, dst, dsnd.at[phase], dsem.at[2 * h + phase], {axis: t})

    def d_first(h):
        recv(R1.at[h], dsem.at[2 * h])
        total = DF[x, :, :, :, lanes[h]] if h == 0 else DF[:, y, :, :, lanes[h]]
        for i in range(3):
            total = total + R1[h, i].astype(F32)
        EF[h] = total
        ES[h] = total.astype(BF16)
        d_start(h, 1)

    def d_second(h):
        recv(R2.at[h], dsem.at[2 * h + 1])
        total = EF[h, pos[order[1 - h]]]
        for i in range(3):
            total = total + R2[h, i].astype(F32)
        PJ[x, y, :, :, lanes[h]] = total.astype(BF16)

    @pl.when(k == 0)
    def _():
        tell(0)
        loads[1].wait()
        gv[0].start(0)
        loads[0].wait()
        gp.start()
        send(VT.at[x, y, :, low], VT.at[x, y, :, low], xsnd.at[1], xrcv.at[1], sib)
        loads[2].wait()
        gq[0].start()
        recv(QT.at[z, 1], xrcv.at[0])
        gq[1].start()
        gp.leaves(0)
        send(b_h, BX, xsnd.at[2], xrcv.at[2], sib)
        send(PT.at[z, 0], PT.at[z, 0], xsnd.at[0], xrcv.at[0], sib)
        send(QT.at[z, 0], QT.at[z, 0], xsnd.at[5], xrcv.at[5], sib)
        loads[3].wait()
        recv(UU.at[x, y, 1], xrcv.at[1])
        hear(0)
        tell(1)
        q_step(0)
        hear(1)
        tell(2)
        q_step(1)
        hear(2)
        pl.semaphore_signal(known, inc=1, device_id=sib, device_id_type=MESH)
        q_step(2)
        both(gu, "start", 0)
        q_step(3)

        @pl.when(diag)
        def _():
            recv(VS, xrcv.at[3])
            scatter_some(close, VS, scsnd)

        q_step(4)

        both(gu, "wait", 0)
        both(gu, "start", 1)
        recv(PT.at[z, 1], xrcv.at[5])
        gp.shared(0)
        q_step(5)

        loads[5].wait()
        recv(AX, xrcv.at[2])
        gp.shared(1)
        d_part(0)
        d_start(0, 0)
        d_part(1)
        d_start(1, 0)
        q_step(6)
        d_first(0)
        d_first(1)
        q_step(7)
        both(gu, "wait", 1)
        send(UU.at[:, :, 1], UN, xsnd.at[4], xrcv.at[4], sib)
        U[...] = UU[:, :, 0].reshape(512, 512).T
        d_second(0)
        d_second(1)
        pl.semaphore_wait(free, 1)
        both(gj, "start", 0)
        for g in gj:
            g.wait(0)
            g.start(1)
        loads[6].wait()
        loads[4].wait()
        for h in (0, 1):
            gj[h].wait(1)
            send(PJ.at[:, :, 1, :, lanes[h]], PN.at[:, :, :, lanes[h]], xsnd.at[6 + h], xrcv.at[6 + h], sib)
        tiles(ACC, C, PJ[:, :, 0].reshape(512, 512), QT)
        recv(WT.at[z], xrcv.at[4])
        for g in gw:
            g.shared(0)
        for g in gw:
            g.shared(1)
        tiles(OUT, ACC, U[...], WT)
        for g in gq:
            g.done()
        sent(PT.at[pl.ds(0, 2)], psnd)
        sent(VT.at[0, pl.ds(0, 3), :, low], vsnd.at[0])
        plane_done(UU, usnd)
        plane_done(PJ, jsnd)
        sent(R1, dsnd.at[0])
        sent(R2, dsnd.at[1])
        sent(PT.at[z, 0], xsnd.at[0])
        sent(VT.at[x, y, :, low], xsnd.at[1])
        sent(BX, xsnd.at[2])
        sent(QT.at[z, 0], xsnd.at[5])
        sent(UN, xsnd.at[4])
        for h in (0, 1):
            sent(PN.at[:, :, :, lanes[h]], xsnd.at[6 + h])

        @pl.when(diag)
        def _():
            sent(PT.at[pl.ds(0, 9)], scsnd)


def per_device(a, b, c, u, v, p, q):
    dma = pltpu.SemaphoreType.DMA
    anywhere = pl.BlockSpec(memory_space=pltpu.HBM)
    vm = pltpu.VMEM
    scratch = [
        vm((16, 2, 16, 1024), BF16),
        vm((16, 2, 16, 1024), BF16),
        vm((4, 4, 32, 1024), BF16),
        vm((4, 4, 32, 1024), BF16),
        vm((4, 4, 2, 32, 512), BF16),
        vm((4, 4, 32, 512), BF16),
        vm((512, 512), BF16),
        *[vm((512, 1024), BF16) for _ in range(5)],
        vm((16, 32, 1024), F32),
        *[vm((n, 32, 1024), BF16) for n in (4, 4, 3, 3, 4, 4, 4, 4)],
        vm((16, 2, 16, 1024), BF16),
        vm((32, 1024), BF16),
        vm((4, 4, 32, 512), BF16),
        vm((4, 4, 2, 32, 512), F32),
        vm((4, 4, 2, 32, 512), BF16),
        vm((2, 3, 4, 2, 32, HALF), BF16),
        vm((2, 4, 2, 32, HALF), F32),
        vm((2, 4, 2, 32, HALF), BF16),
        vm((2, 3, 2, 32, HALF), BF16),
        vm((4, 4, 2, 32, 512), BF16),
        vm((4, 4, 32, 512), BF16),
        vm((512, 1024), F32),
        dma((7,)), dma((8,)), dma((8,)),
        dma((15,)), dma, dma((2,)),
        *[dma((2, 15)), dma((2,)), dma((2, 2))] * 2,
        dma((8,)),
        dma((4,)), dma((3,)), dma((4,)), dma((4,)), dma,
        *[dma((4,)), dma((2,))] * 5,
        dma, dma, dma, pltpu.SemaphoreType.REGULAR, pltpu.SemaphoreType.REGULAR, pltpu.SemaphoreType.REGULAR((6,)),
    ]
    return pl.pallas_call(
        kernel,
        out_shape=jax.ShapeDtypeStruct(c.shape, c.dtype),
        in_specs=[anywhere] * 7,
        out_specs=pl.BlockSpec(memory_space=pltpu.VMEM),
        scratch_shapes=scratch,
        compiler_params=pltpu.CompilerParams(
            collective_id=0, has_side_effects=True, vmem_limit_bytes=67043328
        ),
        name="maintain",
    )(v.T, u.T, p.T, q.T, a, b, c)


def solution(mesh):
    split = Mesh(mesh.devices.reshape(NZ, 2, 4, 4), ("z", "k", "x", "y"))
    row, col = ("z", "k"), ("x", "y")
    placed = (
        P(row, col), P(row, col), P(row, col), P(row, col), P(row, col), P(col, row), P(col, row),
    )
    return jax.shard_map(
        per_device, mesh=split, in_specs=placed, out_specs=P(row, col), check_vma=False
    )
```

time: 254 us -> 72.6 us (0.29)
  blocking collectives: 97.8 us -> 0 us
  waiting for transfers between devices: 82.2 us -> 0 us
  Pallas kernels: 0 us -> 70.2 us
  starting transfers between devices: 31 us -> 0 us
  matrix products: 13.3 us -> 0 us
  between operations: 13.3 us -> 0.01 us
  local copies, waits for them, and re-layouts: 11.7 us -> 2.26 us
  other arithmetic: 3.29 us -> 0 us
    all_to_all x4 -> x0, blocking collectives: 72.4 us -> none  [the longest x1 27.1 us: summed_rows(): lax.all_to_all(nearer, far, split_axis=0, concat_axis=0, tiled=True)]
    pallas_call x0 -> x1, Pallas kernels: none -> 70.2 us  [per_device(): pl.pallas_call(kernel, out_shape=jax.ShapeDtypeStruct(c.shape, c.dtype),...]
    all_gather x2 -> x0, waiting for transfers between devices: 61.8 us -> none  [the longest x1 46.2 us: gather_turned(): result = lax.all_gather(both, axis, axis=0, tiled=True)]
    all_to_all x4 -> x0, starting transfers between devices: 30.9 us -> none  [the longest x3 27.2 us: from_everyone(): return lax.all_to_all(copies, axis, split_axis=0, concat_axis=0, tiled=True)]
    all_gather x1 -> x0, blocking collectives: 25.3 us -> none  [all_blocks(): pieces = lax.all_gather(pieces, axes[k], axis=0, tiled=True)]
    dot_general x6 -> x0, matrix products: 13.3 us -> none  [the longest x2 4.65 us: contract_tail(): lax.dot_general(first, second, (((1,), (1,)), ((), ())), preferred_elemen...]
    reduce_scatter x2 -> x0, waiting for transfers between devices: 13.2 us -> none  [sum_in_order(): pieces = lax.psum_scatter(pieces, axes[k], scatter_dimension=0, tiled=True)]
    all_to_all x4 -> x0, waiting for transfers between devices: 7.12 us -> none  [the longest x3 7.12 us: from_everyone(): return lax.all_to_all(copies, axis, split_axis=0, concat_axis=0, tiled=True)]
  transfers between devices with their start and end apart: 8 -> 0, of which waited for: 4 -> 0; matrix products, arithmetic and copies ran while one was open for 9% -> 0% of each run, Pallas kernels for 0% -> 0%
where the time goes in v2:
time: 72.6 us; the launch traced here: 72.5 us
  Pallas kernels  70.2 us (97%)
  local copies, waits for them, and re-layouts  2.26 us (3%)
    pallas_call x1, Pallas kernels, per_device(): pl.pallas_call(kernel, out_shape=jax.ShapeDtypeStruct(c.shape, c.dtype),...  70.2 us
    unnamed x1, local copies, waits for them, and re-layouts  2.26 us

profile of v2, /device:TPU:1, one launch (start us, length us, event | category | flops | bytes accessed | tf_op | source)
XLA Modules:
  0.0 72.5 jit_solution(2997022039932774661)
XLA Ops:
  0.0 70.2 %maintain.1 = bf16[512,1024]{1,0:T(8,128)(2,1)} custom-call(bf16[32,512]{1,0:T(8,128)(2,1)} %bitcast.4, bf16[32,512]{1,0:T(8,128)(2,1)} %bitcast.5, bf16[16,1024]{1,0:T(8,128)(2,1)} %bitcast.6, bf16[16,1024]{1,0:T(8,128)(2,1)} %bitcast.7, bf16[512,1024]{1,0:T(8,128)(2,1)} %a_h.1, bf16[512,1024]{1,0:T(8,128)(2,1)} %b_h.1, bf16[512,1024]{1,0:T(8,128)(2,1)} %c_h.1), custom_call_target="tpu_custom_call" | custom-call | tf_op jit(solution)/shard_map/maintain/pallas_call | solution.py:596
  70.2 2.3 %copy.9 = bf16[512,1024]{1,0:T(8,128)(2,1)} copy(bf16[512,1024]{1,0:T(8,128)(2,1)} %maintain.1) | data formatting | bytes 2097152

commit v3 on v2

--- a/solution.py
+++ b/solution.py
@@ -20,13 +20,13 @@
 
 
 def kernel(
-    vt_h, ut_h, pt_h, qt_h, a_h, b_h, c_h, OUT,
-    PT, QT, VT, VS, UU, UN, U, A, AX, B, BX, C, W,
+    vt_h, ut_h, pt_h, qt_h, a_h, b_h, c_h, out_h,
+    PT, QT, VT, UU, UN, U, A, AX, B, BX, C, W,
     RSP, RRP, RSM, RRM, LSP, LRP, LSM, LRM, WT,
-    XV, CR, DF, DS, R1, EF, ES, R2, PJ, PN, ACC,
-    load_sem, xrcv, xsnd, psem, psnd, pfwd, qsem, qsnd, qfwd, wsem, wsnd, wfwd, phalf,
+    OUT, XV, TV, CR, DF, DS, R1, EF, ES, R2, PJ, PN, ACC,
+    load_sem, xrcv, xsnd, psem, psnd, pfwd, qsem, qsnd, qfwd, wsem, wsnd, wfwd,
     rpr, rmr, lpr, lmr, rsnd, vsem, vsnd, usem, usnd, crsem, crsnd,
-    dsem, dsnd, jsem, jsnd, scsem, scsnd, scfar, free, known, told,
+    dsem, dsnd, jsem, jsnd, scsem, scsnd, tvsem, tusnd, free, known, told,
 ):
     z = lax.axis_index("z")
     k = lax.axis_index("k")
@@ -36,7 +36,9 @@
     zp, zm = {"z": rem(z + 1, NZ)}, {"z": rem(z - 1, NZ)}
     zpp, zmm = {"z": rem(z + 2, NZ)}, {"z": rem(z - 2, NZ)}
     pos = {"x": x, "y": y}
-    diag = z == 4 * x + y
+    c = 4 * x + y
+    gap = rem(c - z, NZ)
+    even = lax.rem(gap, 2) == 0
 
     def send(src, dst, ssem, rsem, dev):
         pltpu.make_async_remote_copy(
@@ -81,8 +83,8 @@
     pl.semaphore_wait(barrier, len(peers))
 
     class ZWide:
-        def __init__(self, buf, rsem, ssem, fwd, part=slice(None)):
-            self.buf, self.rsem, self.ssem, self.fwd, self.part = buf, rsem, ssem, fwd, part
+        def __init__(self, buf, rsem, ssem, fwd, part, to={}):
+            self.buf, self.rsem, self.ssem, self.fwd, self.part, self.to = buf, rsem, ssem, fwd, part, to
 
         def at(self, d):
             return self.buf.at[rem(z - d, NZ), self.part]
@@ -92,7 +94,7 @@
 
         def out(self, ref, d):
             dev = {1: zp, 2: zpp, -1: zm, -2: zmm}[d if abs(d) < 3 else (2 - d % 2) * (1 if d > 0 else -1)]
-            send(ref, ref, self.ssem, self.rsem.at[self.place(d)], dev)
+            send(ref, ref, self.ssem, self.rsem.at[self.place(d)], {**dev, **self.to})
 
         def arrive(self, d):
             ref = self.at(d)
@@ -103,20 +105,13 @@
             ref = self.at(d)
             send(ref, ref, self.ssem, self.fwd.at[0 if abs(d) < 6 else 1], sib)
 
-        def own(self):
-            return self.at(0)
-
         def start(self):
-            self.out(self.own(), 2)
-            self.out(self.own(), -2)
+            self.out(self.at(0), 2)
+            self.out(self.at(0), -2)
 
         def leaves(self, j):
             for sign in (1, -1):
-                self.out(self.at(2 * j * sign) if j else self.own(), (2 * j + 1) * sign)
-
-        def hub(self, j):
-            self.on(j)
-            self.off(j)
+                self.out(self.at(2 * j * sign), (2 * j + 1) * sign)
 
         def on(self, j):
             for sign, most in ((1, 8), (-1, 7)):
@@ -125,8 +120,9 @@
                 if 2 * j + 2 <= most:
                     self.out(ref, d + 2 * sign)
 
-        def off(self, j):
-            self.leaves(j - 1)
+        def off(self, j, skip=False):
+            if not skip:
+                self.leaves(j - 1)
             if j == 3:
                 self.leaves(3)
             self.share(2 * j)
@@ -164,28 +160,6 @@
                         self.out(ref, d + sign)
                     self.share(d)
 
-    class ZHalves(ZWide):
-        def own(self):
-            return self.buf.at[z, k]
-
-        def out(self, ref, d):
-            if abs(d) > 2:
-                super().out(ref, d)
-                return
-            dev = {1: zp, 2: zpp, -1: zm, -2: zmm}[d]
-            place = 4 * k + {1: 0, 2: 1, -1: 2, -2: 3}[d]
-            send(ref, ref, self.ssem, phalf.at[place], {**dev, "k": 1})
-
-        def arrive(self, d):
-            if abs(d) > 2:
-                return super().arrive(d)
-            for kk in (0, 1):
-                recv(self.buf.at[rem(z - d, NZ), kk], phalf.at[4 * kk + {1: 0, 2: 1, -1: 2, -2: 3}[d]])
-            return self.at(d)
-
-        def done(self):
-            sent(W.at[pl.ds(0, 14)], self.ssem)
-
     class PlaneGather:
         def __init__(self, buf, lanes, first, rsem, ssem, base, to):
             self.buf, self.lanes, self.first = buf, lanes, first
@@ -225,7 +199,7 @@
         sent(buf.at[0, pl.ds(0, 3)], ssem.at[0])
         sent(buf.at[pl.ds(0, 3)], ssem.at[1])
 
-    gp = ZHalves(PT, psem, psnd, pfwd)
+    gp = [ZWide(PT, psem.at[i], psnd.at[i], pfwd.at[i], i, {"k": 1}) for i in (0, 1)]
     gw = [ZWide(WT, wsem.at[i], wsnd.at[i], wfwd.at[i], i) for i in (0, 1)]
     gq = [ZNear(QT, qsem.at[i], qsnd.at[i], qfwd.at[i], i) for i in (0, 1)]
     gv = halves(VT, vsem, vsnd, [low, high], {"k": 1})
@@ -243,30 +217,46 @@
             weights = right[..., at].reshape(512, HALF)
             part = jnp.dot(left, weights, preferred_element_type=F32)
             dst[:, at] = (base[:, at].astype(F32) + part).astype(dst.dtype)
-
-    def rs_out(d, parts, src, dst, rsem, i, dev):
-        total = W[d]
+            if dst is OUT:
+                result(j).start()
+
+    def result(j):
+        at = pl.ds(j * HALF, HALF)
+        return pltpu.make_async_copy(OUT.at[:, at], out_h.at[:, at], load_sem.at[j])
+
+    def stored():
+        for j in range(4):
+            result(j).wait()
+
+    cols = [low, high]
+
+    def rs_out(d, parts, src, dst, rsem, i, p, dev):
+        total = W[d, :, cols[p]]
         for ref, sem, n in parts:
-            recv(ref.at[n], sem.at[n])
-            total = total + ref[n].astype(F32)
-        src[i] = total.astype(BF16)
-        send(src.at[i], dst.at[i], rsnd, rsem.at[i], dev)
-
-    def rs_plus(i):
+            recv(ref.at[n, :, cols[p]], sem.at[p, n])
+            total = total + ref[n, :, cols[p]].astype(F32)
+        src[i, :, cols[p]] = total.astype(BF16)
+        send(src.at[i, :, cols[p]], dst.at[i, :, cols[p]], rsnd, rsem.at[p, i], dev)
+
+    def rs_plus(i, p):
         parts = [(LRP, lpr, i - 1), (RRP, rpr, i - 1)] if i else []
-        rs_out(rem(z + 8 - 2 * i, NZ), parts, RSP, RRP, rpr, i, zpp)
-
-    def rs_minus(i):
+        rs_out(rem(z + 8 - 2 * i, NZ), parts, RSP, RRP, rpr, i, p, zpp)
+
+    def rs_minus(i, p):
         parts = [(LRM, lmr, i)] + ([(RRM, rmr, i - 1)] if i else [])
-        rs_out(rem(z - 6 + 2 * i, NZ), parts, RSM, RRM, rmr, i, zmm)
-
-    def rs_leaf(i):
-        rs_out(rem(z - 7 + 2 * i, NZ), [], LSM, LRM, lmr, i, zm)
-        rs_out(rem(z + 7 - 2 * i, NZ), [], LSP, LRP, lpr, i, zp)
-
-    def sum_w():
+        rs_out(rem(z - 6 + 2 * i, NZ), parts, RSM, RRM, rmr, i, p, zmm)
+
+    def rs_leaf(i, p):
+        rs_out(rem(z - 7 + 2 * i, NZ), [], LSM, LRM, lmr, i, p, zm)
+        rs_out(rem(z + 7 - 2 * i, NZ), [], LSP, LRP, lpr, i, p, zp)
+
+    def rs_both(what, i):
+        for p in (0, 1):
+            what(i, p)
+
+    def sum_w(p):
         left = VT[...].reshape(512, 1024)
-        for j in range(4):
+        for j in (2 * p, 2 * p + 1):
             at = pl.ds(j * HALF, HALF)
             part = jnp.dot(left[:, :512], BX[:, at], preferred_element_type=F32)
             part = part + jnp.dot(left[:, 512:], B[:, at], preferred_element_type=F32)
@@ -280,9 +270,20 @@
         cross = jnp.sum(CR[...].astype(F32).reshape(16, 32, 512), axis=0).astype(BF16)
         total = W[z] + jnp.dot(cross, QT[...].reshape(512, 1024), preferred_element_type=F32)
         for ref, sem, n in ((LRP, lpr, 3), (LRM, lmr, 3), (RRP, rpr, 3), (RRM, rmr, 2)):
-            recv(ref.at[n], sem.at[n])
+            for p in (0, 1):
+                recv(ref.at[n, :, cols[p]], sem.at[p, n])
             total = total + ref[n].astype(F32)
         WT[z] = total.astype(BF16).reshape(2, 16, 1024)
+
+    def p_hub(j):
+        for g in gp:
+            g.on(j)
+        gp[0].off(j, j == 1)
+        gp[1].off(j)
+
+    def p_leaf(j):
+        for g in gp:
+            g.leaf(j)
 
     def w_start():
         for g in gw:
@@ -314,26 +315,48 @@
         pl.semaphore_wait(told.at[i], 1)
         pl.semaphore_wait(told.at[3 + i], 1)
 
-    far = (8, 7, 9, 6, 10, 5, 11)
-    close = (4, 12, 3, 13, 2, 14, 1, 15, 0)
-
-    def scatter_some(some, src, ssem):
-        for d in some:
-            zz = rem(z + d, NZ)
-            send(src.at[zz // 4, lax.rem(zz, 4)], XV, ssem, scsem, {"z": zz, "k": 1})
-
-    def pass_v():
-        return pltpu.make_async_remote_copy(
-            src_ref=VT, dst_ref=VS, send_sem=xsnd.at[3], recv_sem=xrcv.at[3],
-            device_id=sib, device_id_type=MESH,
-        )
+    def scatter():
+        def one(d):
+            b = rem(z + d, NZ)
+            send(VT.at[b // 4, lax.rem(b, 4)], TV, scsnd, tvsem, {"z": b, "k": 1})
+
+        @pl.when(even & (gap != 0))
+        def _():
+            one(gap // 2)
+
+        @pl.when(even)
+        def _():
+            one(gap // 2 + 8)
+
+    def turn():
+        @pl.when(gap != 0)
+        def _():
+            recv(TV, tvsem)
+
+        @pl.when(lax.rem(gap, 8) != 0)
+        def _():
+            a = rem(2 * z - c, NZ)
+            send(TV, XV, tusnd, scsem, {"k": 1, "x": a // 4, "y": lax.rem(a, 4)})
+
+        @pl.when(gap == 8)
+        def _():
+            XV[...] = TV[...]
+
+        @pl.when(gap == 0)
+        def _():
+            XV[...] = VT[x, y]
+
+    def turned():
+        @pl.when(lax.rem(gap, 8) != 0)
+        def _():
+            recv(XV, scsem)
 
     @pl.when(k == 1)
     def _():
         loads[1].wait()
         gv[1].start(0)
         loads[0].wait()
-        gp.start()
+        gp[1].start()
         loads[2].wait()
         send(QT.at[z, 1], QT.at[z, 1], xsnd.at[0], xrcv.at[0], sib)
         loads[3].wait()
@@ -342,47 +365,46 @@
         send(a_h, AX, xsnd.at[2], xrcv.at[2], sib)
         gv[1].wait(0)
         gv[1].start(1)
+        p_hub(1)
         recv(VT.at[x, y, :, low], xrcv.at[1])
         gv[0].wait(0)
         gv[0].start(1)
-        gp.hub(1)
-        gp.hub(2)
-        gp.leaf(0)
+        p_hub(2)
+        p_leaf(0)
         gv[1].wait(1)
         gv[0].wait(1)
-
         pl.semaphore_wait(known, 1)
 
-        @pl.when(diag)
-        def _():
-            pass_v().start()
-            scatter_some(far, VT, scfar)
+        scatter()
 
         loads[4].wait()
         recv(BX, xrcv.at[2])
-        sum_w()
-        rs_plus(0)
-        rs_leaf(0)
-        gp.hub(3)
-        gp.leaf(1)
-        gp.leaf(2)
-        rs_minus(0)
-        rs_leaf(1)
-        gp.last()
-        gp.leaf(3)
-        rs_plus(1)
-        rs_minus(1)
-        rs_leaf(2)
+        for p in (0, 1):
+            sum_w(p)
+            rs_plus(0, p)
+            rs_leaf(0, p)
+        p_hub(3)
+        p_leaf(1)
+        rs_both(rs_minus, 0)
+        rs_both(rs_leaf, 1)
+        rs_both(rs_plus, 1)
+        turn()
+        rs_both(rs_minus, 1)
+        rs_both(rs_leaf, 2)
+        p_leaf(2)
+        for g in gp:
+            g.last()
+        p_leaf(3)
         recv(PT.at[z, 0], xrcv.at[0])
-        recv(XV, scsem)
+        turned()
         cross_part()
         both(gc, "start", 0)
-        rs_plus(2)
-        rs_minus(2)
-        rs_leaf(3)
+        rs_both(rs_plus, 2)
         both(gc, "wait", 0)
         both(gc, "start", 1)
-        rs_plus(3)
+        rs_both(rs_minus, 2)
+        rs_both(rs_leaf, 3)
+        rs_both(rs_plus, 3)
         recv(QT.at[z, 0], xrcv.at[5])
         for g in gq:
             g.shared(0)
@@ -408,8 +430,8 @@
         w_last()
         w_leaf(3)
         tiles(OUT, ACC, U[...], WT)
-        gp.done()
-        for g in gw:
+        sent(PT.at[pl.ds(0, 13)], psnd.at[0])
+        for g in (gp[1], *gw):
             g.done()
         sent(PT.at[pl.ds(0, 15)], rsnd)
         sent(VT.at[0, pl.ds(0, 3), :, low], vsnd.at[0])
@@ -421,10 +443,19 @@
         sent(WT.at[z], xsnd.at[4])
         sent(PT.at[z, 1], xsnd.at[5])
 
-        @pl.when(diag)
-        def _():
-            pass_v().wait_send()
-            sent(PT.at[pl.ds(0, 7)], scfar)
+        @pl.when(even & (gap != 0))
+        def _():
+            sent(PT.at[pl.ds(0, 2)], scsnd)
+
+        @pl.when(gap == 0)
+        def _():
+            sent(PT.at[0], scsnd)
+
+        @pl.when(lax.rem(gap, 8) != 0)
+        def _():
+            sent(TV, tusnd)
+
+        stored()
 
 
     def d_part(h):
@@ -467,13 +498,13 @@
         loads[1].wait()
         gv[0].start(0)
         loads[0].wait()
-        gp.start()
+        gp[0].start()
         send(VT.at[x, y, :, low], VT.at[x, y, :, low], xsnd.at[1], xrcv.at[1], sib)
         loads[2].wait()
         gq[0].start()
         recv(QT.at[z, 1], xrcv.at[0])
         gq[1].start()
-        gp.leaves(0)
+        gp[0].leaves(0)
         send(b_h, BX, xsnd.at[2], xrcv.at[2], sib)
         send(PT.at[z, 0], PT.at[z, 0], xsnd.at[0], xrcv.at[0], sib)
         send(QT.at[z, 0], QT.at[z, 0], xsnd.at[5], xrcv.at[5], sib)
@@ -488,43 +519,37 @@
         hear(2)
         pl.semaphore_signal(known, inc=1, device_id=sib, device_id_type=MESH)
         q_step(2)
-        both(gu, "start", 0)
         q_step(3)
 
-        @pl.when(diag)
-        def _():
-            recv(VS, xrcv.at[3])
-            scatter_some(close, VS, scsnd)
-
         q_step(4)
-
-        both(gu, "wait", 0)
-        both(gu, "start", 1)
         recv(PT.at[z, 1], xrcv.at[5])
-        gp.shared(0)
-        q_step(5)
-
+        for g in gp:
+            g.shared(0)
+            g.shared(1)
         loads[5].wait()
         recv(AX, xrcv.at[2])
-        gp.shared(1)
         d_part(0)
         d_start(0, 0)
         d_part(1)
         d_start(1, 0)
+        both(gu, "start", 0)
+        q_step(5)
         q_step(6)
         d_first(0)
         d_first(1)
+        both(gu, "wait", 0)
+        both(gu, "start", 1)
         q_step(7)
-        both(gu, "wait", 1)
-        send(UU.at[:, :, 1], UN, xsnd.at[4], xrcv.at[4], sib)
-        U[...] = UU[:, :, 0].reshape(512, 512).T
         d_second(0)
         d_second(1)
         pl.semaphore_wait(free, 1)
         both(gj, "start", 0)
+        both(gu, "wait", 1)
+        send(UU.at[:, :, 1], UN, xsnd.at[4], xrcv.at[4], sib)
         for g in gj:
             g.wait(0)
             g.start(1)
+        U[...] = UU[:, :, 0].reshape(512, 512).T
         loads[6].wait()
         loads[4].wait()
         for h in (0, 1):
@@ -539,7 +564,7 @@
         tiles(OUT, ACC, U[...], WT)
         for g in gq:
             g.done()
-        sent(PT.at[pl.ds(0, 2)], psnd)
+        sent(PT.at[pl.ds(0, 2)], psnd.at[0])
         sent(VT.at[0, pl.ds(0, 3), :, low], vsnd.at[0])
         plane_done(UU, usnd)
         plane_done(PJ, jsnd)
@@ -552,10 +577,7 @@
         sent(UN, xsnd.at[4])
         for h in (0, 1):
             sent(PN.at[:, :, :, lanes[h]], xsnd.at[6 + h])
-
-        @pl.when(diag)
-        def _():
-            sent(PT.at[pl.ds(0, 9)], scsnd)
+        stored()
 
 
 def per_device(a, b, c, u, v, p, q):
@@ -566,7 +588,6 @@
         vm((16, 2, 16, 1024), BF16),
         vm((16, 2, 16, 1024), BF16),
         vm((4, 4, 32, 1024), BF16),
-        vm((4, 4, 32, 1024), BF16),
         vm((4, 4, 2, 32, 512), BF16),
         vm((4, 4, 32, 512), BF16),
         vm((512, 512), BF16),
@@ -574,6 +595,8 @@
         vm((16, 32, 1024), F32),
         *[vm((n, 32, 1024), BF16) for n in (4, 4, 3, 3, 4, 4, 4, 4)],
         vm((16, 2, 16, 1024), BF16),
+        vm((512, 1024), BF16),
+        vm((32, 1024), BF16),
         vm((32, 1024), BF16),
         vm((4, 4, 32, 512), BF16),
         vm((4, 4, 2, 32, 512), F32),
@@ -586,18 +609,16 @@
         vm((4, 4, 32, 512), BF16),
         vm((512, 1024), F32),
         dma((7,)), dma((8,)), dma((8,)),
-        dma((15,)), dma, dma((2,)),
-        *[dma((2, 15)), dma((2,)), dma((2, 2))] * 2,
-        dma((8,)),
-        dma((4,)), dma((3,)), dma((4,)), dma((4,)), dma,
+        *[dma((2, 15)), dma((2,)), dma((2, 2))] * 3,
+        dma((2, 4)), dma((2, 3)), dma((2, 4)), dma((2, 4)), dma,
         *[dma((4,)), dma((2,))] * 5,
-        dma, dma, dma, pltpu.SemaphoreType.REGULAR, pltpu.SemaphoreType.REGULAR, pltpu.SemaphoreType.REGULAR((6,)),
+        dma, dma, dma, dma, pltpu.SemaphoreType.REGULAR, pltpu.SemaphoreType.REGULAR, pltpu.SemaphoreType.REGULAR((6,)),
     ]
     return pl.pallas_call(
         kernel,
         out_shape=jax.ShapeDtypeStruct(c.shape, c.dtype),
         in_specs=[anywhere] * 7,
-        out_specs=pl.BlockSpec(memory_space=pltpu.VMEM),
+        out_specs=anywhere,
         scratch_shapes=scratch,
         compiler_params=pltpu.CompilerParams(
             collective_id=0, has_side_effects=True, vmem_limit_bytes=67043328

time: 72.6 us -> 68.4 us (0.942)
  Pallas kernels: 70.2 us -> 66 us
    pallas_call x1, Pallas kernels: 70.2 us -> 66 us  [per_device(): pl.pallas_call(kernel, out_shape=jax.ShapeDtypeStruct(c.shape, c.dtype),...]
where the time goes in v3:
time: 68.4 us; the launch traced here: 68.2 us
  Pallas kernels  66 us (96%)
  local copies, waits for them, and re-layouts  2.26 us (3%)
    pallas_call x1, Pallas kernels, per_device(): pl.pallas_call(kernel, out_shape=jax.ShapeDtypeStruct(c.shape, c.dtype),...  66 us
    unnamed x1, local copies, waits for them, and re-layouts  2.26 us

profile of v3, /device:TPU:1, one launch (start us, length us, event | category | flops | bytes accessed | tf_op | source)
XLA Modules:
  0.0 68.2 jit_solution(10741660853403121123)
XLA Ops:
  0.0 66.0 %maintain.1 = bf16[512,1024]{1,0:T(8,128)(2,1)} custom-call(bf16[32,512]{1,0:T(8,128)(2,1)} %bitcast.4, bf16[32,512]{1,0:T(8,128)(2,1)} %bitcast.5, bf16[16,1024]{1,0:T(8,128)(2,1)} %bitcast.6, bf16[16,1024]{1,0:T(8,128)(2,1)} %bitcast.7, bf16[512,1024]{1,0:T(8,128)(2,1)} %a_h.1, bf16[512,1024]{1,0:T(8,128)(2,1)} %b_h.1, bf16[512,1024]{1,0:T(8,128)(2,1)} %c_h.1), custom_call_target="tpu_custom_call" | custom-call | tf_op jit(solution)/shard_map/maintain/pallas_call | solution.py:617
  66.0 2.3 %copy.9 = bf16[512,1024]{1,0:T(8,128)(2,1)} copy(bf16[512,1024]{1,0:T(8,128)(2,1)} %maintain.1) | data formatting | bytes 2097152

commit v4 on v3

--- a/solution.py
+++ b/solution.py
@@ -513,12 +513,15 @@
         hear(0)
         tell(1)
         q_step(0)
+        both(gu, "start", 0)
         hear(1)
         tell(2)
         q_step(1)
         hear(2)
         pl.semaphore_signal(known, inc=1, device_id=sib, device_id_type=MESH)
         q_step(2)
+        both(gu, "wait", 0)
+        both(gu, "start", 1)
         q_step(3)
 
         q_step(4)
@@ -532,13 +535,10 @@
         d_start(0, 0)
         d_part(1)
         d_start(1, 0)
-        both(gu, "start", 0)
         q_step(5)
         q_step(6)
         d_first(0)
         d_first(1)
-        both(gu, "wait", 0)
-        both(gu, "start", 1)
         q_step(7)
         d_second(0)
         d_second(1)

time: 68.4 us -> 67.5 us (0.987)
  Pallas kernels: 66 us -> 65 us
    pallas_call x1, Pallas kernels: 66 us -> 65 us  [per_device(): pl.pallas_call(kernel, out_shape=jax.ShapeDtypeStruct(c.shape, c.dtype),...]
where the time goes in v4:
time: 67.5 us; the launch traced here: 67.3 us
  Pallas kernels  65 us (96%)
  local copies, waits for them, and re-layouts  2.26 us (3%)
    pallas_call x1, Pallas kernels, per_device(): pl.pallas_call(kernel, out_shape=jax.ShapeDtypeStruct(c.shape, c.dtype),...  65 us
    unnamed x1, local copies, waits for them, and re-layouts  2.26 us

profile of v4, /device:TPU:1, one launch (start us, length us, event | category | flops | bytes accessed | tf_op | source)
XLA Modules:
  0.0 67.3 jit_solution(12053030282891961830)
XLA Ops:
  0.0 65.0 %maintain.1 = bf16[512,1024]{1,0:T(8,128)(2,1)} custom-call(bf16[32,512]{1,0:T(8,128)(2,1)} %bitcast.4, bf16[32,512]{1,0:T(8,128)(2,1)} %bitcast.5, bf16[16,1024]{1,0:T(8,128)(2,1)} %bitcast.6, bf16[16,1024]{1,0:T(8,128)(2,1)} %bitcast.7, bf16[512,1024]{1,0:T(8,128)(2,1)} %a_h.1, bf16[512,1024]{1,0:T(8,128)(2,1)} %b_h.1, bf16[512,1024]{1,0:T(8,128)(2,1)} %c_h.1), custom_call_target="tpu_custom_call" | custom-call | tf_op jit(solution)/shard_map/maintain/pallas_call | solution.py:617
  65.0 2.3 %copy.9 = bf16[512,1024]{1,0:T(8,128)(2,1)} copy(bf16[512,1024]{1,0:T(8,128)(2,1)} %maintain.1) | data formatting | bytes 2097152
